TPU v7x, 32 devices: a whole 2x2x4 slice. The times are simulated.
32 devices in a mesh: dp: 16 (over z, y, core), tensor: 2 (over x).
Axes of the slice: x: 2, y: 2, z: 4, core: 2. Of those that a mesh axis runs over, the one named last changes fastest.
Arguments:
- activations: bfloat16 [32768, 1024], P(('dp', 'tensor')), may hold values from -6 to 6
- gradients: bfloat16 [32768, 5472], P('dp', 'tensor'), may hold values from -6 to 6
- act_history: float32 [2, 16, 1024], P('tensor'), may hold values from 0.1 to 4
- grad_history: float32 [16, 5472], P(None, 'tensor'), may hold values from 0.1 to 4
- owner_rank: int32 [1024], replicated, may hold values from 0 to 1
- history_slot: int32 [6496], replicated, may hold values from 0 to 15
Outputs:
- weight_grad: float32 [1024, 5472], P('dp', 'tensor')
- act_history_out: float32 [2, 16, 1024], P('tensor')
- grad_history_out: float32 [16, 5472], P(None, 'tensor')
All inputs are finite; a program needn't handle non-finite values.
Results may differ from a plain program's by a relative error of at most 0.0042.
Values may be sent and summed in bfloat16 or wider, within the bound.
No kernel may reach another device: no remote copies, remote signals or barrier semaphores. Data moves between devices by JAX's collectives and lax.ppermute only.
A program may use at most 64 MiB of HBM per device.

v0:
```python
import math

import jax
import jax.numpy as jnp
from jax import lax
from jax.experimental.layout import Layout, with_layout_constraint
from jax.sharding import PartitionSpec as P

QUANT_LIMIT = 448.0
SCALE_FLOOR = 0.25


def quantize(values, scale):
    scaled = values.astype(jnp.float32) * scale
    return jnp.clip(scaled, -QUANT_LIMIT, QUANT_LIMIT).astype(jnp.bfloat16)


def place_peaks(history, peaks, slots):
    rows = lax.broadcasted_iota(jnp.int32, history.shape, 0)
    return jnp.where(rows == slots[None, :], peaks[None, :], history)


def shifted(values, axis, shift):
    size = lax.axis_size(axis)
    return lax.ppermute(values, axis, [(i, (i + shift) % size) for i in range(size)])


def butterfly_max(values, axis):
    size = lax.axis_size(axis)
    if size & (size - 1):
        return lax.pmax(values, axis)
    step = 1
    while step < size:
        other = lax.ppermute(values, axis, [(i, i ^ step) for i in range(size)])
        values = jnp.maximum(values, other)
        step *= 2
    return values


def after(values, *others):
    return lax.optimization_barrier((values,) + others)[0]


def row_major(values):
    return with_layout_constraint(values, Layout(major_to_minor=(0, 1)))


def body(activations, gradients, act_history, grad_history, owner_rank, history_slot):
    model_width = act_history.shape[2]
    token_rows = activations.shape[0]
    column_total = gradients.shape[1]
    tensor_size = lax.axis_size("tensor")
    dp_size = lax.axis_size("dp")
    my_rank = lax.axis_index("tensor")
    my_dp = lax.axis_index("dp")
    plane_count = dp_size // 4
    rows = model_width // dp_size
    plane_width = 4 * rows
    my_core = my_dp % 2
    my_y = (my_dp // 2) % 2
    my_plane = my_dp // 4
    grad_factor = 1.0 / math.sqrt(gradients.shape[0] * dp_size)

    planes = [(my_plane + 1 + k) % plane_count for k in range(plane_count)]

    def plane_of(values, plane, axis):
        return lax.dynamic_slice_in_dim(values, plane * plane_width, plane_width, axis)

    history = act_history[0]
    histories = [shifted(history, "tensor", shift) for shift in range(1, tensor_size)]
    pieces = [plane_of(activations, plane, 1) for plane in planes]
    received = []
    for piece in pieces:
        received.append([shifted(piece, "tensor", shift) for shift in range(1, tensor_size)])
    current_history = jnp.where(owner_rank[None, :] == my_rank, act_history[0], jnp.float32(0.0))
    for shift in range(1, tensor_size):
        source = (my_rank - shift) % tensor_size
        current_history = jnp.where(
            owner_rank[None, :] == source, histories[shift - 1], current_history
        )

    act_scale = QUANT_LIMIT / jnp.maximum(jnp.max(current_history, axis=0), SCALE_FLOOR)
    grad_scale = QUANT_LIMIT / jnp.maximum(jnp.max(grad_history, axis=0), SCALE_FLOOR)
    act_scale, grad_scale = lax.optimization_barrier((act_scale, grad_scale))

    def token_block(rank):
        block = lax.dynamic_slice_in_dim(gradients, rank * token_rows, token_rows, 0)
        return quantize(block, grad_scale)

    own_grad = token_block(my_rank)
    other_grad = jnp.concatenate(
        [token_block((my_rank - shift) % tensor_size) for shift in range(1, tensor_size)],
        axis=0,
    )
    own_grad, other_grad = lax.optimization_barrier((own_grad, other_grad))
    contract_rows = (((0,), (0,)), ((), ()))

    def product(left, right):
        result = lax.dot_general(left, right, contract_rows, preferred_element_type=jnp.float32)
        return row_major(result)

    core_pairs = [(i, i ^ 1) for i in range(dp_size)]
    y_pairs = [(i, i ^ 2) for i in range(dp_size)]
    scales = [plane_of(act_scale, plane, 0) for plane in planes]
    own_parts = []
    for k, piece in enumerate(pieces):
        own_part = product(quantize(piece, scales[k]), own_grad)
        own_parts.append(lax.optimization_barrier(own_part))

    def split(part):
        def block(y, core):
            return lax.dynamic_slice_in_dim(part, (2 * y + core) * rows, rows, 0)

        def exchange(y):
            away = row_major(block(y, 1 - my_core).astype(jnp.bfloat16))
            return lax.ppermute(lax.optimization_barrier(away), "dp", core_pairs)

        landed = (exchange(1 - my_y), exchange(my_y))

        def of(own_chip, *others):
            y = my_y if own_chip else 1 - my_y
            return block(y, my_core) + widen(after(landed[own_chip], *others))

        return of

    def widen(values):
        return values.astype(jnp.float32)

    def send_plane(k, total):
        hop = 4 * (k + 1)
        pairs = [(i, (i + hop) % dp_size) for i in range(dp_size)]
        return lax.ppermute(total, "dp", pairs)

    own_act_peak = jnp.max(jnp.abs(activations), axis=0)
    own_grad_peak = jnp.max(jnp.abs(after(gradients, own_grad)), axis=0)
    own_act_peak, own_grad_peak = lax.optimization_barrier((own_act_peak, own_grad_peak))
    own_act_peak = own_act_peak.astype(jnp.float32)
    own_grad_peak = own_grad_peak.astype(jnp.float32)
    peaks = jnp.concatenate([own_act_peak, own_grad_peak])
    peak_steps = [1 << bit for bit in range(dp_size.bit_length() - 1)]

    def partner_peaks(k, values):
        step = peak_steps[k]
        return lax.ppermute(values, "dp", [(i, i ^ step) for i in range(dp_size)])

    other_peaks = partner_peaks(0, peaks)
    peak_count = 1

    arrivals = []
    state = None
    ready = ()
    for k in range(plane_count):
        remote = jnp.concatenate(received[k], axis=0) if tensor_size > 2 else received[k][0]
        part = product(quantize(after(remote, *ready), scales[k]), other_grad) + own_parts[k]
        of = split(lax.optimization_barrier(part))
        to_neighbour = lax.optimization_barrier(row_major(of(False).astype(jnp.bfloat16)))
        from_neighbour = lax.ppermute(to_neighbour, "dp", y_pairs)
        ready = (to_neighbour,)
        if state is not None:
            of_last, from_last = state
            total = of_last(True) + widen(after(from_last, to_neighbour))
            total = lax.optimization_barrier(row_major(total.astype(jnp.bfloat16)))
            arrivals.append(send_plane(k - 1, total))
            ready = (to_neighbour, total)
        state = (of, from_neighbour)
        if peak_count < len(peak_steps):
            peaks = jnp.maximum(peaks, after(other_peaks, to_neighbour))
            other_peaks = partner_peaks(peak_count, peaks)
            peak_count += 1
    peaks = jnp.maximum(peaks, after(other_peaks, to_neighbour))
    while peak_count < len(peak_steps):
        peaks = jnp.maximum(peaks, partner_peaks(peak_count, peaks))
        peak_count += 1
    act_peak = butterfly_max(peaks[:model_width], "tensor")
    grad_peak = peaks[model_width:]
    of_last, from_last = state
    summed = of_last(True) + widen(from_last)
    for arrival in arrivals:
        summed = summed + widen(arrival)

    act_peak, grad_peak, current_history, grad_history = lax.optimization_barrier(
        (act_peak, grad_peak, current_history, grad_history)
    )

    row_scale = lax.dynamic_slice_in_dim(act_scale, my_dp * rows, rows, 0)
    weight_grad = summed / (row_scale[:, None] * grad_scale[None, :]) * grad_factor
    act_slots = history_slot[:model_width]
    grad_slots = lax.dynamic_slice_in_dim(
        history_slot, model_width + my_rank * column_total, column_total, 0
    )
    act_history_out = place_peaks(current_history, act_peak, act_slots)[None]
    grad_history_out = place_peaks(grad_history, grad_peak, grad_slots)
    return (weight_grad, act_history_out, grad_history_out)


def solution(mesh):
    placed = (
        P(("dp", "tensor"), None),
        P("dp", "tensor"),
        P("tensor", None, None),
        P(None, "tensor"),
        P(),
        P(),
    )

    return jax.shard_map(
        body,
        mesh=mesh,
        in_specs=placed,
        out_specs=(P("dp", "tensor"), P("tensor", None, None), P(None, "tensor")),
        check_vma=False,
    )
```

profile of v0, /device:TPU:0, one launch (start us, length us, event | category | flops | bytes accessed | tf_op | source)
XLA Modules:
  0.0 125.5 jit_solution(980524042988854488)
XLA Ops:
  0.7 3.0 %collective-permute-start.4 = (f32[16,1024]{1,0:T(8,128)}, f32[16,1024]{1,0:T(8,128)S(1)}, u32[]{:S(2)}, u32[]{:S(2)}) collective-permute-start(f32[16,1024]{1,0:T(8,128)} %bitcast.13), channel_id=1, source_target_pairs={{0,1},{1,0},{2,3},{3,2},{4,5},{5,4},{6,7},{7,6},{8,9},{9,8},{10,11... | collective-permute-start | bytes 196616 | tf_op jit(solution)/shard_map/ppermute | solution.py:25
  3.7 2.9 %constant_dynamic-slice_fusion.3 = (bf16[1024,256]{1,0:T(8,128)(2,1)}, bf16[1024,256]{1,0:T(8,128)(2,1)}, bf16[1024,256]{1,0:T(8,128)(2,1)}, bf16[1024,256]{1,0:T(8,128)(2,1)}) fusion(bf16[1024,1024]{1,0:T(8,128)(2,1)} %param.6, s32[]{:T(128)S(6)} %select_n.110, s32[]{:T(128)S(6)} %select_n.114, s32[]{:T(128)S(6)} %select_n.112, s32[]{:T(128)S(6)} %select_n.116), kind=kLoop, calls=%fused_computation.70 | loop fusion | bytes 4194320 | tf_op jit(solution)/shard_map/dynamic_slice | solution.py:67
  6.9 1.8 %collective-permute-start.2 = (bf16[1024,256]{1,0:T(8,128)(2,1)}, bf16[1024,256]{1,0:T(8,128)(2,1)S(1)}, u32[]{:S(2)}, u32[]{:S(2)}) collective-permute-start(bf16[1024,256]{1,0:T(8,128)(2,1)} %get-tuple-element.58), channel_id=1, source_target_pairs={{0,1},{1,0},{2,3},{3,2},{4,5},{5,4},{6,7},{7,6},{8,9},{9,8},{10,11... | collective-permute-start | bytes 1572872 | tf_op jit(solution)/shard_map/ppermute | solution.py:25
  8.9 1.8 %collective-permute-start = (bf16[1024,256]{1,0:T(8,128)(2,1)}, bf16[1024,256]{1,0:T(8,128)(2,1)}, u32[]{:S(2)}, u32[]{:S(2)}) collective-permute-start(bf16[1024,256]{1,0:T(8,128)(2,1)} %get-tuple-element.57), channel_id=1, source_target_pairs={{0,1},{1,0},{2,3},{3,2},{4,5},{5,4},{6,7},{7,6},{8,9},{9,8},{10,11... | collective-permute-start | bytes 1572872 | tf_op jit(solution)/shard_map/ppermute | solution.py:25
  11.2 6.2 %clamp_convert_fusion = (bf16[1024,2736]{0,1:T(8,128)(2,1)S(1)}, bf16[1024,2736]{0,1:T(8,128)(2,1)S(1)}) fusion(bf16[2048,2736]{0,1:T(8,128)(2,1)} %param.7, s32[]{:T(128)S(6)} %select_n.121, f32[2736]{0:T(1024)S(1)} %maximum_divide_fusion, s32[]{:T(128)S(6)} %select_n.120), kind=kLoop, calls=%fused_computation.1 | loop fusion | flops 22413312 | bytes 22424264 | tf_op jit(solution)/shard_map/convert_element_type | solution.py:15
  17.4 2.4 %copy-done.2 = bf16[1024,2736]{0,1:T(8,128)(2,1)} copy-done((bf16[1024,2736]{0,1:T(8,128)(2,1)}, bf16[1024,2736]{0,1:T(8,128)(2,1)S(1)}, u32[]{:S(2)}) %copy-start.2) | copy-done | bytes 5603352
  19.9 2.8 %fusion = f32[256,2736]{1,0:T(8,128)S(1)} fusion(bf16[1024,2736]{0,1:T(8,128)(2,1)S(1)} %get-tuple-element.27, bf16[1024,256]{1,0:T(8,128)(2,1)} %get-tuple-element.60, f32[256]{0:T(256)S(1)} %get-tuple-element.64), kind=kOutput, calls=%fused_computation.32 | convolution fusion | flops 1435500544 | bytes 8930304 | tf_op jit(solution)/shard_map/dot_general | solution.py:99
  22.7 6.5 %abs_reduce_fusion = bf16[2736]{0:T(1024)(128)(2,1)S(1)} fusion(bf16[2048,2736]{0,1:T(8,128)(2,1)} %param.7), kind=kLoop, calls=%fused_computation | loop fusion | flops 11203920 | bytes 11212128 | tf_op jit(solution)/shard_map/reduce_max | solution.py:135
  29.1 3.0 %convolution_add_fusion.3 = f32[256,2736]{1,0:T(8,128)S(1)} fusion(f32[256,2736]{1,0:T(8,128)S(1)} %fusion, bf16[1024,2736]{0,1:T(8,128)(2,1)S(1)} %get-tuple-element.26, bf16[1024,256]{1,0:T(8,128)(2,1)} %collective-permute-done.3, f32[256]{0:T(256)S(1)} %get-tuple-element.64), kind=kOutput, calls=%fused_computation.6 | convolution fusion | flops 1436200960 | bytes 11731968 | tf_op jit(solution)/shard_map/dot_general | solution.py:99
  32.3 2.8 %fusion.1 = f32[256,2736]{1,0:T(8,128)S(1)} fusion(bf16[1024,2736]{0,1:T(8,128)(2,1)S(1)} %copy-done.3, bf16[1024,256]{1,0:T(8,128)(2,1)} %get-tuple-element.58, f32[256]{0:T(256)S(1)} %get-tuple-element.63), kind=kOutput, calls=%fused_computation.33 | convolution fusion | flops 1435500544 | bytes 8930304 | tf_op jit(solution)/shard_map/dot_general | solution.py:99
  35.7 1.8 %convolution_add_fusion.2 = f32[256,2736]{1,0:T(8,128)S(1)} fusion(f32[256,2736]{1,0:T(8,128)S(1)} %fusion.1, bf16[1024,2736]{0,1:T(8,128)(2,1)S(1)} %get-tuple-element.26, bf16[1024,256]{1,0:T(8,128)(2,1)S(1)} %collective-permute-done.2, f32[256]{0:T(256)S(1)} %get-tuple-element.63), kind=kOutput, calls=%fused_computation.5 | convolution fusion | flops 1436200960 | bytes 11731968 | tf_op jit(solution)/shard_map/dot_general | solution.py:99
  37.8 2.8 %fusion.2 = f32[256,2736]{1,0:T(8,128)S(1)} fusion(bf16[1024,2736]{0,1:T(8,128)(2,1)S(1)} %copy-done.3, bf16[1024,256]{1,0:T(8,128)(2,1)} %get-tuple-element.59, f32[256]{0:T(256)S(1)} %get-tuple-element.62), kind=kOutput, calls=%fused_computation.34 | convolution fusion | flops 1435500544 | bytes 8930304 | tf_op jit(solution)/shard_map/dot_general | solution.py:99
  40.6 1.6 %collective-permute-start.8 = (bf16[64,2736]{1,0:T(8,128)(2,1)S(1)}, bf16[64,2736]{1,0:T(8,128)(2,1)S(1)}, u32[]{:S(2)}, u32[]{:S(2)}) collective-permute-start(bf16[64,2736]{1,0:T(8,128)(2,1)S(1)} %add_convert_fusion.6), channel_id=1, source_target_pairs={{0,4},{2,6},{4,0},{6,2},{8,12},{10,14},{12,8},{14,10},{16,20},{18,... | collective-permute-start | bytes 1050632 | tf_op jit(solution)/shard_map/ppermute | solution.py:157
  42.4 9.0 %collective-permute-done.8 = bf16[64,2736]{1,0:T(8,128)(2,1)S(1)} collective-permute-done((bf16[64,2736]{1,0:T(8,128)(2,1)S(1)}, bf16[64,2736]{1,0:T(8,128)(2,1)S(1)}, u32[]{:S(2)}, u32[]{:S(2)}) %collective-permute-start.8) | collective-permute-done | bytes 350240 | tf_op jit(solution)/shard_map/ppermute | solution.py:157
  51.6 3.1 %convolution_add_fusion.1 = f32[256,2736]{1,0:T(8,128)S(1)} fusion(f32[256,2736]{1,0:T(8,128)S(1)} %fusion.2, bf16[1024,2736]{0,1:T(8,128)(2,1)S(1)} %get-tuple-element.26, bf16[1024,256]{1,0:T(8,128)(2,1)} %collective-permute-done.1, f32[256]{0:T(256)S(1)} %get-tuple-element.62), kind=kOutput, calls=%fused_computation.4 | convolution fusion | flops 1436200960 | bytes 11731968 | tf_op jit(solution)/shard_map/dot_general | solution.py:99
  55.5 2.8 %fusion.3 = f32[256,2736]{1,0:T(8,128)S(1)} fusion(bf16[1024,2736]{0,1:T(8,128)(2,1)S(1)} %copy-done.3, bf16[1024,256]{1,0:T(8,128)(2,1)} %get-tuple-element.57, f32[256]{0:T(256)S(1)} %get-tuple-element.61), kind=kOutput, calls=%fused_computation.35 | convolution fusion | flops 1435500544 | bytes 8930304 | tf_op jit(solution)/shard_map/dot_general | solution.py:99
  58.3 1.6 %collective-permute-start.11 = (bf16[64,2736]{1,0:T(8,128)(2,1)S(1)}, bf16[64,2736]{1,0:T(8,128)(2,1)S(1)}, u32[]{:S(2)}, u32[]{:S(2)}) collective-permute-start(bf16[64,2736]{1,0:T(8,128)(2,1)S(1)} %add_convert_fusion.5), channel_id=1, source_target_pairs={{0,4},{2,6},{4,0},{6,2},{8,12},{10,14},{12,8},{14,10},{16,20},{18,... | collective-permute-start | bytes 1050632 | tf_op jit(solution)/shard_map/ppermute | solution.py:157
  60.9 8.3 %collective-permute-done.11 = bf16[64,2736]{1,0:T(8,128)(2,1)S(1)} collective-permute-done((bf16[64,2736]{1,0:T(8,128)(2,1)S(1)}, bf16[64,2736]{1,0:T(8,128)(2,1)S(1)}, u32[]{:S(2)}, u32[]{:S(2)}) %collective-permute-start.11) | collective-permute-done | bytes 350240 | tf_op jit(solution)/shard_map/ppermute | solution.py:157
  70.0 2.8 %convolution_add_fusion = f32[256,2736]{1,0:T(8,128)S(1)} fusion(f32[256,2736]{1,0:T(8,128)S(1)} %fusion.3, bf16[1024,2736]{0,1:T(8,128)(2,1)S(1)} %get-tuple-element.26, bf16[1024,256]{1,0:T(8,128)(2,1)} %collective-permute-done, f32[256]{0:T(256)S(1)} %get-tuple-element.61), kind=kOutput, calls=%fused_computation.3 | convolution fusion | flops 1436200960 | bytes 11731968 | tf_op jit(solution)/shard_map/dot_general | solution.py:99
  72.9 1.6 %copy-done = f32[256,2736]{1,0:T(8,128)} copy-done((f32[256,2736]{1,0:T(8,128)}, f32[256,2736]{1,0:T(8,128)S(1)}, u32[]{:S(2)}) %copy-start) | copy-done | bytes 2801688
  75.9 1.5 %collective-permute-done.20 = f32[3760]{0:T(1024)S(1)} collective-permute-done((f32[3760]{0:T(1024)S(1)}, f32[3760]{0:T(1024)S(1)}, u32[]{:S(2)}, u32[]{:S(2)}) %collective-permute-start.20) | collective-permute-done | bytes 15072 | tf_op jit(solution)/shard_map/ppermute | solution.py:144
  77.4 1.5 %collective-permute-start.21 = (f32[3760]{0:T(1024)S(1)}, f32[3760]{0:T(1024)S(1)}, u32[]{:S(2)}, u32[]{:S(2)}) collective-permute-start(f32[3760]{0:T(1024)S(1)} %fusion.29), channel_id=1, source_target_pairs={{0,4},{2,6},{4,0},{6,2},{8,12},{10,14},{12,8},{14,10},{16,20},{18,... | collective-permute-start | bytes 45128 | tf_op jit(solution)/shard_map/ppermute | solution.py:144
  79.0 2.2 %collective-permute-done.21 = f32[3760]{0:T(1024)S(1)} collective-permute-done((f32[3760]{0:T(1024)S(1)}, f32[3760]{0:T(1024)S(1)}, u32[]{:S(2)}, u32[]{:S(2)}) %collective-permute-start.21) | collective-permute-done | bytes 15072 | tf_op jit(solution)/shard_map/ppermute | solution.py:144
  81.2 1.6 %collective-permute-start.22 = (f32[3760]{0:T(1024)S(1)}, f32[3760]{0:T(1024)S(1)}, u32[]{:S(2)}, u32[]{:S(2)}) collective-permute-start(f32[3760]{0:T(1024)S(1)} %max.62), channel_id=1, source_target_pairs={{0,8},{2,10},{4,12},{6,14},{8,0},{10,2},{12,4},{14,6},{16,24},{18,... | collective-permute-start | bytes 45128 | tf_op jit(solution)/shard_map/ppermute | solution.py:144
  84.1 1.5 %collective-permute-start.18 = (bf16[64,2736]{1,0:T(8,128)(2,1)}, bf16[64,2736]{1,0:T(8,128)(2,1)S(1)}, u32[]{:S(2)}, u32[]{:S(2)}) collective-permute-start(bf16[64,2736]{1,0:T(8,128)(2,1)} %add_convert_fusion.3), channel_id=1, source_target_pairs={{0,4},{2,6},{4,0},{6,2},{8,12},{10,14},{12,8},{14,10},{16,20},{18,... | collective-permute-start | bytes 1050632 | tf_op jit(solution)/shard_map/ppermute | solution.py:157
  85.6 2.6 %collective-permute-start.16 = (bf16[64,2736]{1,0:T(8,128)(2,1)}, bf16[64,2736]{1,0:T(8,128)(2,1)S(1)}, u32[]{:S(2)}, u32[]{:S(2)}) collective-permute-start(bf16[64,2736]{1,0:T(8,128)(2,1)} %add_convert_fusion.2), channel_id=1, source_target_pairs={{0,16},{2,18},{4,20},{6,22},{8,24},{10,26},{12,28},{14,30},{16,0},... | collective-permute-start | bytes 1050632 | tf_op jit(solution)/shard_map/ppermute | solution.py:132
  88.6 1.3 %add_convert_fusion.1 = bf16[64,2736]{1,0:T(8,128)(2,1)S(1)} fusion(bf16[64,2736]{1,0:T(8,128)(2,1)} %collective-permute-done.13, f32[256,2736]{1,0:T(8,128)} %copy-done, s32[]{:T(128)S(6)} %select_n.125), kind=kLoop, calls=%fused_computation.19 | loop fusion | flops 525312 | bytes 1400836 | tf_op jit(solution)/shard_map/convert_element_type | solution.py:156
  89.9 20.9 %collective-permute-done.23 = f32[3760]{0:T(1024)S(1)} collective-permute-done((f32[3760]{0:T(1024)S(1)}, f32[3760]{0:T(1024)S(1)}, u32[]{:S(2)}, u32[]{:S(2)}) %collective-permute-start.23) | collective-permute-done | bytes 15072 | tf_op jit(solution)/shard_map/ppermute | solution.py:144
  110.8 1.1 collective-permute-start.14
  113.7 2.0 %collective-permute-start.19 = (bf16[64,2736]{1,0:T(8,128)(2,1)S(1)}, bf16[64,2736]{1,0:T(8,128)(2,1)S(1)}, u32[]{:S(2)}, u32[]{:S(2)}) collective-permute-start(bf16[64,2736]{1,0:T(8,128)(2,1)S(1)} %add_convert_fusion), channel_id=1, source_target_pairs={{0,24},{2,26},{4,28},{6,30},{8,0},{10,2},{12,4},{14,6},{16,8},{18,... | collective-permute-start | bytes 1050632 | tf_op jit(solution)/shard_map/ppermute | solution.py:132
  117.0 6.1 %collective-permute-done.19 = bf16[64,2736]{1,0:T(8,128)(2,1)S(1)} collective-permute-done((bf16[64,2736]{1,0:T(8,128)(2,1)S(1)}, bf16[64,2736]{1,0:T(8,128)(2,1)S(1)}, u32[]{:S(2)}, u32[]{:S(2)}) %collective-permute-start.19) | collective-permute-done | bytes 350240 | tf_op jit(solution)/shard_map/ppermute | solution.py:132
  123.2 2.3 %divide_multiply_fusion = f32[64,2736]{1,0:T(8,128)} fusion(bf16[64,2736]{1,0:T(8,128)(2,1)S(1)} %collective-permute-done.19, bf16[64,2736]{1,0:T(8,128)(2,1)S(1)} %collective-permute-done.16, bf16[64,2736]{1,0:T(8,128)(2,1)S(1)} %collective-permute-done.15, bf16[64,2736]{1,0:T(8,128)(2,1)S(1)} %collective-permute-done.14, ...), kind=kLoop, calls=%fused_computation.16 | loop fusion | flops 2276352 | bytes 3163076 | tf_op jit(solution)/shard_map/mul | solution.py:186
  (76 shorter events, 11.3 us)
Async XLA Ops:
  0.6 10.5 %copy-start.5 = (f32[1,16,1024]{2,1,0:T(8,128)S(1)}, f32[1,16,1024]{2,1,0:T(8,128)}, u32[]{:S(2)}) copy-start(f32[1,16,1024]{2,1,0:T(8,128)} %param.8) | copy-start | bytes 196612
  0.6 10.1 %copy-start.1 = (bf16[1024,1024]{1,0:T(8,128)(2,1)S(1)}, bf16[1024,1024]{1,0:T(8,128)(2,1)}, u32[]{:S(2)}) copy-start(bf16[1024,1024]{1,0:T(8,128)(2,1)} %param.6) | copy-start | bytes 6291460
  0.7 10.3 %copy-start.4 = (f32[16,2736]{1,0:T(8,128)S(1)}, f32[16,2736]{1,0:T(8,128)}, u32[]{:S(2)}) copy-start(f32[16,2736]{1,0:T(8,128)} %param.9) | copy-start | bytes 525316
  0.7 10.3 %copy-start.6 = (s32[1024]{0:T(1024)S(1)}, s32[1024]{0:T(1024)}, u32[]{:S(2)}) copy-start(s32[1024]{0:T(1024)} %param.10) | copy-start | bytes 12292
  0.7 10.4 %collective-permute-start.4 = (f32[16,1024]{1,0:T(8,128)}, f32[16,1024]{1,0:T(8,128)S(1)}, u32[]{:S(2)}, u32[]{:S(2)}) collective-permute-start(f32[16,1024]{1,0:T(8,128)} %bitcast.13), channel_id=1, source_target_pairs={{0,1},{1,0},{2,3},{3,2},{4,5},{5,4},{6,7},{7,6},{8,9},{9,8},{10,11... | collective-permute-start | bytes 196616 | tf_op jit(solution)/shard_map/ppermute | solution.py:25
  6.6 22.5 %collective-permute-start.3 = (bf16[1024,256]{1,0:T(8,128)(2,1)}, bf16[1024,256]{1,0:T(8,128)(2,1)}, u32[]{:S(2)}, u32[]{:S(2)}) collective-permute-start(bf16[1024,256]{1,0:T(8,128)(2,1)} %get-tuple-element.60), channel_id=1, source_target_pairs={{0,1},{1,0},{2,3},{3,2},{4,5},{5,4},{6,7},{7,6},{8,9},{9,8},{10,11... | collective-permute-start | bytes 1572872 | tf_op jit(solution)/shard_map/ppermute | solution.py:25
  6.9 28.8 %collective-permute-start.2 = (bf16[1024,256]{1,0:T(8,128)(2,1)}, bf16[1024,256]{1,0:T(8,128)(2,1)S(1)}, u32[]{:S(2)}, u32[]{:S(2)}) collective-permute-start(bf16[1024,256]{1,0:T(8,128)(2,1)} %get-tuple-element.58), channel_id=1, source_target_pairs={{0,1},{1,0},{2,3},{3,2},{4,5},{5,4},{6,7},{7,6},{8,9},{9,8},{10,11... | collective-permute-start | bytes 1572872 | tf_op jit(solution)/shard_map/ppermute | solution.py:25
  8.7 42.9 %collective-permute-start.1 = (bf16[1024,256]{1,0:T(8,128)(2,1)}, bf16[1024,256]{1,0:T(8,128)(2,1)}, u32[]{:S(2)}, u32[]{:S(2)}) collective-permute-start(bf16[1024,256]{1,0:T(8,128)(2,1)} %get-tuple-element.59), channel_id=1, source_target_pairs={{0,1},{1,0},{2,3},{3,2},{4,5},{5,4},{6,7},{7,6},{8,9},{9,8},{10,11... | collective-permute-start | bytes 1572872 | tf_op jit(solution)/shard_map/ppermute | solution.py:25
  8.9 61.1 %collective-permute-start = (bf16[1024,256]{1,0:T(8,128)(2,1)}, bf16[1024,256]{1,0:T(8,128)(2,1)}, u32[]{:S(2)}, u32[]{:S(2)}) collective-permute-start(bf16[1024,256]{1,0:T(8,128)(2,1)} %get-tuple-element.57), channel_id=1, source_target_pairs={{0,1},{1,0},{2,3},{3,2},{4,5},{5,4},{6,7},{7,6},{8,9},{9,8},{10,11... | collective-permute-start | bytes 1572872 | tf_op jit(solution)/shard_map/ppermute | solution.py:25
  17.4 2.4 %copy-start.2 = (bf16[1024,2736]{0,1:T(8,128)(2,1)}, bf16[1024,2736]{0,1:T(8,128)(2,1)S(1)}, u32[]{:S(2)}) copy-start(bf16[1024,2736]{0,1:T(8,128)(2,1)S(1)} %get-tuple-element.27) | copy-start | bytes 16809988
  29.1 3.2 %copy-start.3 = (bf16[1024,2736]{0,1:T(8,128)(2,1)S(1)}, bf16[1024,2736]{0,1:T(8,128)(2,1)}, u32[]{:S(2)}) copy-start(bf16[1024,2736]{0,1:T(8,128)(2,1)} %copy-done.2) | copy-start | bytes 16809988
  32.2 3.5 %collective-permute-start.5 = (bf16[64,2736]{1,0:T(8,128)(2,1)S(1)}, bf16[64,2736]{1,0:T(8,128)(2,1)S(1)}, u32[]{:S(2)}, u32[]{:S(2)}) collective-permute-start(bf16[64,2736]{1,0:T(8,128)(2,1)S(1)} %get-tuple-element.56), channel_id=1, source_target_pairs={{0,2},{2,0},{4,6},{6,4},{8,10},{10,8},{12,14},{14,12},{16,18},{18,... | collective-permute-start | bytes 1050632 | tf_op jit(solution)/shard_map/ppermute | solution.py:116
  35.1 7.1 %collective-permute-start.7 = (bf16[64,2736]{1,0:T(8,128)(2,1)S(1)}, bf16[64,2736]{1,0:T(8,128)(2,1)S(1)}, u32[]{:S(2)}, u32[]{:S(2)}) collective-permute-start(bf16[64,2736]{1,0:T(8,128)(2,1)S(1)} %get-tuple-element.55), channel_id=1, source_target_pairs={{0,2},{2,0},{4,6},{6,4},{8,10},{10,8},{12,14},{14,12},{16,18},{18,... | collective-permute-start | bytes 1050632 | tf_op jit(solution)/shard_map/ppermute | solution.py:116
  37.7 4.7 %collective-permute-start.6 = (bf16[64,2736]{1,0:T(8,128)(2,1)S(1)}, bf16[64,2736]{1,0:T(8,128)(2,1)S(1)}, u32[]{:S(2)}, u32[]{:S(2)}) collective-permute-start(bf16[64,2736]{1,0:T(8,128)(2,1)S(1)} %get-tuple-element.54), channel_id=1, source_target_pairs={{0,2},{2,0},{4,6},{6,4},{8,10},{10,8},{12,14},{14,12},{16,18},{18,... | collective-permute-start | bytes 1050632 | tf_op jit(solution)/shard_map/ppermute | solution.py:116
  40.6 10.9 %collective-permute-start.8 = (bf16[64,2736]{1,0:T(8,128)(2,1)S(1)}, bf16[64,2736]{1,0:T(8,128)(2,1)S(1)}, u32[]{:S(2)}, u32[]{:S(2)}) collective-permute-start(bf16[64,2736]{1,0:T(8,128)(2,1)S(1)} %add_convert_fusion.6), channel_id=1, source_target_pairs={{0,4},{2,6},{4,0},{6,2},{8,12},{10,14},{12,8},{14,10},{16,20},{18,... | collective-permute-start | bytes 1050632 | tf_op jit(solution)/shard_map/ppermute | solution.py:157
  42.2 17.9 %collective-permute-start.10 = (bf16[64,2736]{1,0:T(8,128)(2,1)S(1)}, bf16[64,2736]{1,0:T(8,128)(2,1)S(1)}, u32[]{:S(2)}, u32[]{:S(2)}) collective-permute-start(bf16[64,2736]{1,0:T(8,128)(2,1)S(1)} %get-tuple-element.53), channel_id=1, source_target_pairs={{0,2},{2,0},{4,6},{6,4},{8,10},{10,8},{12,14},{14,12},{16,18},{18,... | collective-permute-start | bytes 1050632 | tf_op jit(solution)/shard_map/ppermute | solution.py:116
  55.5 4.6 %collective-permute-start.9 = (bf16[64,2736]{1,0:T(8,128)(2,1)S(1)}, bf16[64,2736]{1,0:T(8,128)(2,1)S(1)}, u32[]{:S(2)}, u32[]{:S(2)}) collective-permute-start(bf16[64,2736]{1,0:T(8,128)(2,1)S(1)} %get-tuple-element.52), channel_id=1, source_target_pairs={{0,2},{2,0},{4,6},{6,4},{8,10},{10,8},{12,14},{14,12},{16,18},{18,... | collective-permute-start | bytes 1050632 | tf_op jit(solution)/shard_map/ppermute | solution.py:116
  58.3 10.9 %collective-permute-start.11 = (bf16[64,2736]{1,0:T(8,128)(2,1)S(1)}, bf16[64,2736]{1,0:T(8,128)(2,1)S(1)}, u32[]{:S(2)}, u32[]{:S(2)}) collective-permute-start(bf16[64,2736]{1,0:T(8,128)(2,1)S(1)} %add_convert_fusion.5), channel_id=1, source_target_pairs={{0,4},{2,6},{4,0},{6,2},{8,12},{10,14},{12,8},{14,10},{16,20},{18,... | collective-permute-start | bytes 1050632 | tf_op jit(solution)/shard_map/ppermute | solution.py:157
  59.9 28.3 %collective-permute-start.17 = (bf16[64,2736]{1,0:T(8,128)(2,1)}, bf16[64,2736]{1,0:T(8,128)(2,1)}, u32[]{:S(2)}, u32[]{:S(2)}) collective-permute-start(bf16[64,2736]{1,0:T(8,128)(2,1)} %get-tuple-element.51), channel_id=1, source_target_pairs={{0,2},{2,0},{4,6},{6,4},{8,10},{10,8},{12,14},{14,12},{16,18},{18,... | collective-permute-start | bytes 1050632 | tf_op jit(solution)/shard_map/ppermute | solution.py:116
  70.0 46.4 %slice-start = ((s32[6496]{0:T(1024)}), s32[1024]{0:T(1024)S(1)}, s32[]{:S(2)}) async-start(s32[6496]{0:T(1024)} %param.11), calls=%async_computation | async-start | bytes 8192 | tf_op jit(solution)/shard_map/slice | solution.py:187
  75.4 13.2 %collective-permute-start.13 = (bf16[64,2736]{1,0:T(8,128)(2,1)}, bf16[64,2736]{1,0:T(8,128)(2,1)}, u32[]{:S(2)}, u32[]{:S(2)}) collective-permute-start(bf16[64,2736]{1,0:T(8,128)(2,1)} %get-tuple-element.50), channel_id=1, source_target_pairs={{0,2},{2,0},{4,6},{6,4},{8,10},{10,8},{12,14},{14,12},{16,18},{18,... | collective-permute-start | bytes 1050632 | tf_op jit(solution)/shard_map/ppermute | solution.py:116
  75.4 2.0 %collective-permute-start.20 = (f32[3760]{0:T(1024)S(1)}, f32[3760]{0:T(1024)S(1)}, u32[]{:S(2)}, u32[]{:S(2)}) collective-permute-start(f32[3760]{0:T(1024)S(1)} %maximum_convert_fusion), channel_id=1, source_target_pairs={{0,2},{2,0},{4,6},{6,4},{8,10},{10,8},{12,14},{14,12},{16,18},{18,... | collective-permute-start | bytes 45128 | tf_op jit(solution)/shard_map/ppermute | solution.py:144
  77.4 3.7 %collective-permute-start.21 = (f32[3760]{0:T(1024)S(1)}, f32[3760]{0:T(1024)S(1)}, u32[]{:S(2)}, u32[]{:S(2)}) collective-permute-start(f32[3760]{0:T(1024)S(1)} %fusion.29), channel_id=1, source_target_pairs={{0,4},{2,6},{4,0},{6,2},{8,12},{10,14},{12,8},{14,10},{16,20},{18,... | collective-permute-start | bytes 45128 | tf_op jit(solution)/shard_map/ppermute | solution.py:144
  81.2 4.4 %collective-permute-start.22 = (f32[3760]{0:T(1024)S(1)}, f32[3760]{0:T(1024)S(1)}, u32[]{:S(2)}, u32[]{:S(2)}) collective-permute-start(f32[3760]{0:T(1024)S(1)} %max.62), channel_id=1, source_target_pairs={{0,8},{2,10},{4,12},{6,14},{8,0},{10,2},{12,4},{14,6},{16,24},{18,... | collective-permute-start | bytes 45128 | tf_op jit(solution)/shard_map/ppermute | solution.py:144
  83.6 33.4 %collective-permute-start.15 = (bf16[64,2736]{1,0:T(8,128)(2,1)S(1)}, bf16[64,2736]{1,0:T(8,128)(2,1)S(1)}, u32[]{:S(2)}, u32[]{:S(2)}) collective-permute-start(bf16[64,2736]{1,0:T(8,128)(2,1)S(1)} %add_convert_fusion.4), channel_id=1, source_target_pairs={{0,8},{2,10},{4,12},{6,14},{8,16},{10,18},{12,20},{14,22},{16,24},... | collective-permute-start | bytes 1050632 | tf_op jit(solution)/shard_map/ppermute | solution.py:132
  84.1 27.9 %collective-permute-start.18 = (bf16[64,2736]{1,0:T(8,128)(2,1)}, bf16[64,2736]{1,0:T(8,128)(2,1)S(1)}, u32[]{:S(2)}, u32[]{:S(2)}) collective-permute-start(bf16[64,2736]{1,0:T(8,128)(2,1)} %add_convert_fusion.3), channel_id=1, source_target_pairs={{0,4},{2,6},{4,0},{6,2},{8,12},{10,14},{12,8},{14,10},{16,20},{18,... | collective-permute-start | bytes 1050632 | tf_op jit(solution)/shard_map/ppermute | solution.py:157
  85.6 31.4 %collective-permute-start.16 = (bf16[64,2736]{1,0:T(8,128)(2,1)}, bf16[64,2736]{1,0:T(8,128)(2,1)S(1)}, u32[]{:S(2)}, u32[]{:S(2)}) collective-permute-start(bf16[64,2736]{1,0:T(8,128)(2,1)} %add_convert_fusion.2), channel_id=1, source_target_pairs={{0,16},{2,18},{4,20},{6,22},{8,24},{10,26},{12,28},{14,30},{16,0},... | collective-permute-start | bytes 1050632 | tf_op jit(solution)/shard_map/ppermute | solution.py:132
  88.2 22.6 %collective-permute-start.23 = (f32[3760]{0:T(1024)S(1)}, f32[3760]{0:T(1024)S(1)}, u32[]{:S(2)}, u32[]{:S(2)}) collective-permute-start(f32[3760]{0:T(1024)S(1)} %max.63), channel_id=1, source_target_pairs={{0,16},{2,18},{4,20},{6,22},{8,24},{10,26},{12,28},{14,30},{16,0},... | collective-permute-start | bytes 45128 | tf_op jit(solution)/shard_map/ppermute | solution.py:144
  88.6 25.1 %collective-permute-start.12 = (bf16[64,2736]{1,0:T(8,128)(2,1)}, bf16[64,2736]{1,0:T(8,128)(2,1)S(1)}, u32[]{:S(2)}, u32[]{:S(2)}) collective-permute-start(bf16[64,2736]{1,0:T(8,128)(2,1)} %get-tuple-element.49), channel_id=1, source_target_pairs={{0,2},{2,0},{4,6},{6,4},{8,10},{10,8},{12,14},{14,12},{16,18},{18,... | collective-permute-start | bytes 1050632 | tf_op jit(solution)/shard_map/ppermute | solution.py:116
  110.8 12.4 %collective-permute-start.14 = (bf16[64,2736]{1,0:T(8,128)(2,1)S(1)}, bf16[64,2736]{1,0:T(8,128)(2,1)S(1)}, u32[]{:S(2)}, u32[]{:S(2)}) collective-permute-start(bf16[64,2736]{1,0:T(8,128)(2,1)S(1)} %add_convert_fusion.1), channel_id=1, source_target_pairs={{0,4},{2,6},{4,0},{6,2},{8,12},{10,14},{12,8},{14,10},{16,20},{18,... | collective-permute-start | bytes 1050632 | tf_op jit(solution)/shard_map/ppermute | solution.py:157
  111.9 3.8 %collective-permute-start.24 = (f32[1024]{0:T(1024)S(1)}, f32[1024]{0:T(1024)S(1)}, u32[]{:S(2)}, u32[]{:S(2)}) collective-permute-start(f32[1024]{0:T(1024)S(1)} %slice.12), channel_id=1, source_target_pairs={{0,1},{1,0},{2,3},{3,2},{4,5},{5,4},{6,7},{7,6},{8,9},{9,8},{10,11... | collective-permute-start | bytes 12296 | tf_op jit(solution)/shard_map/ppermute | solution.py:34
  113.7 9.5 %collective-permute-start.19 = (bf16[64,2736]{1,0:T(8,128)(2,1)S(1)}, bf16[64,2736]{1,0:T(8,128)(2,1)S(1)}, u32[]{:S(2)}, u32[]{:S(2)}) collective-permute-start(bf16[64,2736]{1,0:T(8,128)(2,1)S(1)} %add_convert_fusion), channel_id=1, source_target_pairs={{0,24},{2,26},{4,28},{6,30},{8,0},{10,2},{12,4},{14,6},{16,8},{18,... | collective-permute-start | bytes 1050632 | tf_op jit(solution)/shard_map/ppermute | solution.py:132
  (1 other events, 1.6 us)
where the time goes:
time: 126 us
  waiting for transfers between devices  48.1 us (38%)
  starting transfers between devices  23.8 us (19%)
  matrix products  21.9 us (17%)
  other arithmetic  20.9 us (17%)
  local copies, waits for them, and re-layouts  9.87 us (8%)
    ppermute x4, waiting for transfers between devices, partner_peaks(): return lax.ppermute(values, 'dp', [(i, i ^ step) for i in range(dp_size)])  24.6 us
    dot_general x8, matrix products, product(): lax.dot_general(left, right, contract_rows, preferred_element_type=jnp.fl...  21.9 us
    ppermute x4, waiting for transfers between devices, body(): from_neighbour = lax.ppermute(to_neighbour, 'dp', y_pairs)  17.3 us
    ppermute x5, starting transfers between devices, shifted(): lax.ppermute(values, axis, [(i, (i + shift) % size) for i in range(size)])  7.08 us
    reduce_max x1, other arithmetic, body(): own_grad_peak = jnp.max(jnp.abs(after(gradients, own_grad)), axis=0)  6.48 us
    convert_element_type x1, other arithmetic, quantize(): return jnp.clip(scaled, -QUANT_LIMIT, QUANT_LIMIT).astype(jnp.bfloat16)  6.16 us
    ppermute x3, waiting for transfers between devices, send_plane(): return lax.ppermute(total, 'dp', pairs)  6.14 us
    ppermute x4, starting transfers between devices, body(): from_neighbour = lax.ppermute(to_neighbour, 'dp', y_pairs)  5.85 us
  transfers between devices with their start and end apart: 25, of which 6 were waited for; matrix products, arithmetic and copies ran while one was open for 37% of the time, Pallas kernels for 0%

commit v1 on v0

--- a/solution.py
+++ b/solution.py
@@ -61,7 +61,9 @@
     my_plane = my_dp // 4
     grad_factor = 1.0 / math.sqrt(gradients.shape[0] * dp_size)
 
-    planes = [(my_plane + 1 + k) % plane_count for k in range(plane_count)]
+    half = plane_count // 2
+    hops = sorted(range(1, plane_count), key=lambda hop: abs(hop - half)) + [0]
+    planes = [(my_plane + hop) % plane_count for hop in hops]
 
     def plane_of(values, plane, axis):
         return lax.dynamic_slice_in_dim(values, plane * plane_width, plane_width, axis)
@@ -127,8 +129,7 @@
         return values.astype(jnp.float32)
 
     def send_plane(k, total):
-        hop = 4 * (k + 1)
-        pairs = [(i, (i + hop) % dp_size) for i in range(dp_size)]
+        pairs = [(i, (i + 4 * hops[k]) % dp_size) for i in range(dp_size)]
         return lax.ppermute(total, "dp", pairs)
 
     own_act_peak = jnp.max(jnp.abs(activations), axis=0)
@@ -137,7 +138,7 @@
     own_act_peak = own_act_peak.astype(jnp.float32)
     own_grad_peak = own_grad_peak.astype(jnp.float32)
     peaks = jnp.concatenate([own_act_peak, own_grad_peak])
-    peak_steps = [1 << bit for bit in range(dp_size.bit_length() - 1)]
+    peak_steps = [1 << bit for bit in reversed(range(dp_size.bit_length() - 1))]
 
     def partner_peaks(k, values):
         step = peak_steps[k]
@@ -152,11 +153,20 @@
     for k in range(plane_count):
         remote = jnp.concatenate(received[k], axis=0) if tensor_size > 2 else received[k][0]
         part = product(quantize(after(remote, *ready), scales[k]), other_grad) + own_parts[k]
-        of = split(lax.optimization_barrier(part))
-        to_neighbour = lax.optimization_barrier(row_major(of(False).astype(jnp.bfloat16)))
+        part = lax.optimization_barrier(part)
+        of = split(part)
+        total = None
+        last = k + 1 == plane_count
+        if last and state is not None:
+            of_last, from_last = state
+            total = of_last(True) + widen(after(from_last, part))
+            total = lax.optimization_barrier(row_major(total.astype(jnp.bfloat16)))
+            arrivals.append(send_plane(k - 1, total))
+        to_neighbour = of(False, *(() if total is None else (total,)))
+        to_neighbour = lax.optimization_barrier(row_major(to_neighbour.astype(jnp.bfloat16)))
         from_neighbour = lax.ppermute(to_neighbour, "dp", y_pairs)
         ready = (to_neighbour,)
-        if state is not None:
+        if state is not None and not last:
             of_last, from_last = state
             total = of_last(True) + widen(after(from_last, to_neighbour))
             total = lax.optimization_barrier(row_major(total.astype(jnp.bfloat16)))

time: 126 us -> 116 us (0.921)
  the two profiles are of different devices: /device:TPU:0 before, /device:TPU:8 now
where the time goes in v1:
time: 116 us
  waiting for transfers between devices  46.4 us (40%)
  matrix products  21.7 us (19%)
  starting transfers between devices  20.1 us (17%)
  other arithmetic  19.2 us (17%)
  local copies, waits for them, and re-layouts  7.37 us (6%)
    ppermute x3, waiting for transfers between devices, send_plane(): return lax.ppermute(total, 'dp', pairs)  27.6 us
    dot_general x8, matrix products, product(): lax.dot_general(left, right, contract_rows, preferred_element_type=jnp.fl...  21.7 us
    ppermute x4, waiting for transfers between devices, body(): from_neighbour = lax.ppermute(to_neighbour, 'dp', y_pairs)  10.8 us
    ppermute x4, waiting for transfers between devices, partner_peaks(): return lax.ppermute(values, 'dp', [(i, i ^ step) for i in range(dp_size)])  7.91 us
    reduce_max x1, other arithmetic, body(): own_grad_peak = jnp.max(jnp.abs(after(gradients, own_grad)), axis=0)  6.48 us
    ppermute x4, starting transfers between devices, body(): from_neighbour = lax.ppermute(to_neighbour, 'dp', y_pairs)  6.18 us
    convert_element_type x1, other arithmetic, quantize(): return jnp.clip(scaled, -QUANT_LIMIT, QUANT_LIMIT).astype(jnp.bfloat16)  6.16 us
    ppermute x5, starting transfers between devices, shifted(): lax.ppermute(values, axis, [(i, (i + shift) % size) for i in range(size)])  5.61 us
  transfers between devices with their start and end apart: 25, of which 6 were waited for; matrix products, arithmetic and copies ran while one was open for 38% of the time, Pallas kernels for 0%

profile of v1, /device:TPU:8, one launch (start us, length us, event | category | flops | bytes accessed | tf_op | source)
XLA Modules:
  0.0 115.8 jit_solution(8356073856614069659)
XLA Ops:
  0.7 1.6 %collective-permute-start.4 = (f32[16,1024]{1,0:T(8,128)}, f32[16,1024]{1,0:T(8,128)S(1)}, u32[]{:S(2)}, u32[]{:S(2)}) collective-permute-start(f32[16,1024]{1,0:T(8,128)} %bitcast.15), channel_id=1, source_target_pairs={{0,1},{1,0},{2,3},{3,2},{4,5},{5,4},{6,7},{7,6},{8,9},{9,8},{10,11... | collective-permute-start | bytes 196616 | tf_op jit(solution)/shard_map/ppermute | solution.py:25
  2.2 2.9 %constant_dynamic-slice_fusion.3 = (bf16[1024,256]{1,0:T(8,128)(2,1)}, bf16[1024,256]{1,0:T(8,128)(2,1)}, bf16[1024,256]{1,0:T(8,128)(2,1)}, bf16[1024,256]{1,0:T(8,128)(2,1)}) fusion(bf16[1024,1024]{1,0:T(8,128)(2,1)} %param.6, s32[]{:T(128)S(6)} %select_n.110, s32[]{:T(128)S(6)} %select_n.114, s32[]{:T(128)S(6)} %select_n.112, s32[]{:T(128)S(6)} %select_n.116), kind=kLoop, calls=%fused_computation.70 | loop fusion | bytes 4194320 | tf_op jit(solution)/shard_map/dynamic_slice | solution.py:69
  5.7 1.4 %collective-permute-start.2 = (bf16[1024,256]{1,0:T(8,128)(2,1)}, bf16[1024,256]{1,0:T(8,128)(2,1)}, u32[]{:S(2)}, u32[]{:S(2)}) collective-permute-start(bf16[1024,256]{1,0:T(8,128)(2,1)} %get-tuple-element.60), channel_id=1, source_target_pairs={{0,1},{1,0},{2,3},{3,2},{4,5},{5,4},{6,7},{7,6},{8,9},{9,8},{10,11... | collective-permute-start | bytes 1572872 | tf_op jit(solution)/shard_map/ppermute | solution.py:25
  7.8 1.4 %collective-permute-start = (bf16[1024,256]{1,0:T(8,128)(2,1)}, bf16[1024,256]{1,0:T(8,128)(2,1)}, u32[]{:S(2)}, u32[]{:S(2)}) collective-permute-start(bf16[1024,256]{1,0:T(8,128)(2,1)} %get-tuple-element.59), channel_id=1, source_target_pairs={{0,1},{1,0},{2,3},{3,2},{4,5},{5,4},{6,7},{7,6},{8,9},{9,8},{10,11... | collective-permute-start | bytes 1572872 | tf_op jit(solution)/shard_map/ppermute | solution.py:25
  9.7 6.2 %clamp_convert_fusion = (bf16[1024,2736]{0,1:T(8,128)(2,1)S(1)}, bf16[1024,2736]{0,1:T(8,128)(2,1)S(1)}) fusion(bf16[2048,2736]{0,1:T(8,128)(2,1)} %param.7, s32[]{:T(128)S(6)} %select_n.121, f32[2736]{0:T(1024)S(1)} %maximum_divide_fusion, s32[]{:T(128)S(6)} %select_n.120), kind=kLoop, calls=%fused_computation.1 | loop fusion | flops 22413312 | bytes 22424264 | tf_op jit(solution)/shard_map/convert_element_type | solution.py:15
  15.9 2.4 %copy-done.1 = bf16[1024,2736]{0,1:T(8,128)(2,1)} copy-done((bf16[1024,2736]{0,1:T(8,128)(2,1)}, bf16[1024,2736]{0,1:T(8,128)(2,1)S(1)}, u32[]{:S(2)}) %copy-start.1) | copy-done | bytes 5603352
  18.3 2.8 %fusion = f32[256,2736]{1,0:T(8,128)S(1)} fusion(bf16[1024,2736]{0,1:T(8,128)(2,1)S(1)} %get-tuple-element.28, bf16[1024,256]{1,0:T(8,128)(2,1)} %get-tuple-element.62, f32[256]{0:T(256)S(1)} %get-tuple-element.66), kind=kOutput, calls=%fused_computation.32 | convolution fusion | flops 1435500544 | bytes 8930304 | tf_op jit(solution)/shard_map/dot_general | solution.py:101
  21.1 6.5 %abs_reduce_fusion = bf16[2736]{0:T(1024)(128)(2,1)S(1)} fusion(bf16[2048,2736]{0,1:T(8,128)(2,1)} %param.7), kind=kLoop, calls=%fused_computation | loop fusion | flops 11203920 | bytes 11212128 | tf_op jit(solution)/shard_map/reduce_max | solution.py:136
  27.6 2.6 %collective-permute-start.20 = (f32[3760]{0:T(1024)S(1)}, f32[3760]{0:T(1024)S(1)}, u32[]{:S(2)}, u32[]{:S(2)}) collective-permute-start(f32[3760]{0:T(1024)S(1)} %maximum_convert_fusion), channel_id=1, source_target_pairs={{0,16},{2,18},{4,20},{6,22},{8,24},{10,26},{12,28},{14,30},{16,0},... | collective-permute-start | bytes 45128 | tf_op jit(solution)/shard_map/ppermute | solution.py:145
  30.3 2.8 %convolution_add_fusion.3 = f32[256,2736]{1,0:T(8,128)S(1)} fusion(f32[256,2736]{1,0:T(8,128)S(1)} %fusion, bf16[1024,2736]{0,1:T(8,128)(2,1)S(1)} %get-tuple-element.27, bf16[1024,256]{1,0:T(8,128)(2,1)} %collective-permute-done.3, f32[256]{0:T(256)S(1)} %get-tuple-element.66), kind=kOutput, calls=%fused_computation.6 | convolution fusion | flops 1436200960 | bytes 11731968 | tf_op jit(solution)/shard_map/dot_general | solution.py:101
  33.3 2.8 %fusion.1 = f32[256,2736]{1,0:T(8,128)S(1)} fusion(bf16[1024,2736]{0,1:T(8,128)(2,1)S(1)} %bitcast.14, bf16[1024,256]{1,0:T(8,128)(2,1)} %get-tuple-element.60, f32[256]{0:T(256)S(1)} %get-tuple-element.65), kind=kOutput, calls=%fused_computation.33 | convolution fusion | flops 1435500544 | bytes 8930304 | tf_op jit(solution)/shard_map/dot_general | solution.py:101
  36.7 2.8 %convolution_add_fusion.2 = f32[256,2736]{1,0:T(8,128)S(1)} fusion(f32[256,2736]{1,0:T(8,128)S(1)} %fusion.1, bf16[1024,2736]{0,1:T(8,128)(2,1)S(1)} %get-tuple-element.27, bf16[1024,256]{1,0:T(8,128)(2,1)} %collective-permute-done.2, f32[256]{0:T(256)S(1)} %get-tuple-element.65), kind=kOutput, calls=%fused_computation.5 | convolution fusion | flops 1436200960 | bytes 11731968 | tf_op jit(solution)/shard_map/dot_general | solution.py:101
  39.8 2.8 %fusion.2 = f32[256,2736]{1,0:T(8,128)S(1)} fusion(bf16[1024,2736]{0,1:T(8,128)(2,1)S(1)} %bitcast.14, bf16[1024,256]{1,0:T(8,128)(2,1)} %get-tuple-element.61, f32[256]{0:T(256)S(1)} %get-tuple-element.64), kind=kOutput, calls=%fused_computation.34 | convolution fusion | flops 1435500544 | bytes 8930304 | tf_op jit(solution)/shard_map/dot_general | solution.py:101
  42.6 1.6 %collective-permute-start.8 = (bf16[64,2736]{1,0:T(8,128)(2,1)S(1)}, bf16[64,2736]{1,0:T(8,128)(2,1)S(1)}, u32[]{:S(2)}, u32[]{:S(2)}) collective-permute-start(bf16[64,2736]{1,0:T(8,128)(2,1)S(1)} %add_convert_fusion.6), channel_id=1, source_target_pairs={{0,4},{2,6},{4,0},{6,2},{8,12},{10,14},{12,8},{14,10},{16,20},{18,... | collective-permute-start | bytes 1050632 | tf_op jit(solution)/shard_map/ppermute | solution.py:167
  44.8 8.7 %collective-permute-done.8 = bf16[64,2736]{1,0:T(8,128)(2,1)S(1)} collective-permute-done((bf16[64,2736]{1,0:T(8,128)(2,1)S(1)}, bf16[64,2736]{1,0:T(8,128)(2,1)S(1)}, u32[]{:S(2)}, u32[]{:S(2)}) %collective-permute-start.8) | collective-permute-done | bytes 350240 | tf_op jit(solution)/shard_map/ppermute | solution.py:167
  53.5 0.9 add_convert_fusion.4
  54.3 2.0 %convolution_add_fusion.1 = f32[256,2736]{1,0:T(8,128)S(1)} fusion(f32[256,2736]{1,0:T(8,128)S(1)} %fusion.2, bf16[1024,2736]{0,1:T(8,128)(2,1)S(1)} %get-tuple-element.27, bf16[1024,256]{1,0:T(8,128)(2,1)S(1)} %collective-permute-done.1, f32[256]{0:T(256)S(1)} %get-tuple-element.64), kind=kOutput, calls=%fused_computation.4 | convolution fusion | flops 1436200960 | bytes 11731968 | tf_op jit(solution)/shard_map/dot_general | solution.py:101
  56.5 2.8 %fusion.3 = f32[256,2736]{1,0:T(8,128)S(1)} fusion(bf16[1024,2736]{0,1:T(8,128)(2,1)S(1)} %bitcast.14, bf16[1024,256]{1,0:T(8,128)(2,1)} %get-tuple-element.59, f32[256]{0:T(256)S(1)} %get-tuple-element.63), kind=kOutput, calls=%fused_computation.35 | convolution fusion | flops 1435500544 | bytes 8930304 | tf_op jit(solution)/shard_map/dot_general | solution.py:101
  59.3 1.6 %collective-permute-start.11 = (bf16[64,2736]{1,0:T(8,128)(2,1)S(1)}, bf16[64,2736]{1,0:T(8,128)(2,1)S(1)}, u32[]{:S(2)}, u32[]{:S(2)}) collective-permute-start(bf16[64,2736]{1,0:T(8,128)(2,1)S(1)} %add_convert_fusion.5), channel_id=1, source_target_pairs={{0,4},{2,6},{4,0},{6,2},{8,12},{10,14},{12,8},{14,10},{16,20},{18,... | collective-permute-start | bytes 1050632 | tf_op jit(solution)/shard_map/ppermute | solution.py:167
  61.6 1.6 %collective-permute-start.15 = (bf16[64,2736]{1,0:T(8,128)(2,1)S(1)}, bf16[64,2736]{1,0:T(8,128)(2,1)S(1)}, u32[]{:S(2)}, u32[]{:S(2)}) collective-permute-start(bf16[64,2736]{1,0:T(8,128)(2,1)S(1)} %add_convert_fusion.3), channel_id=1, source_target_pairs={{0,4},{2,6},{4,0},{6,2},{8,12},{10,14},{12,8},{14,10},{16,20},{18,... | collective-permute-start | bytes 1050632 | tf_op jit(solution)/shard_map/ppermute | solution.py:167
  63.1 7.9 %collective-permute-done.22 = f32[3760]{0:T(1024)S(1)} collective-permute-done((f32[3760]{0:T(1024)S(1)}, f32[3760]{0:T(1024)S(1)}, u32[]{:S(2)}, u32[]{:S(2)}) %collective-permute-start.22) | collective-permute-done | bytes 15072 | tf_op jit(solution)/shard_map/ppermute | solution.py:145
  71.1 0.9 add_convert_fusion.2
  71.9 2.8 %convolution_add_fusion = f32[256,2736]{1,0:T(8,128)S(1)} fusion(f32[256,2736]{1,0:T(8,128)S(1)} %fusion.3, bf16[1024,2736]{0,1:T(8,128)(2,1)S(1)} %get-tuple-element.27, bf16[1024,256]{1,0:T(8,128)(2,1)} %collective-permute-done, f32[256]{0:T(256)S(1)} %get-tuple-element.63), kind=kOutput, calls=%fused_computation.3 | convolution fusion | flops 1436200960 | bytes 11731968 | tf_op jit(solution)/shard_map/dot_general | solution.py:101
  76.1 2.2 %collective-permute-done.15 = bf16[64,2736]{1,0:T(8,128)(2,1)S(1)} collective-permute-done((bf16[64,2736]{1,0:T(8,128)(2,1)S(1)}, bf16[64,2736]{1,0:T(8,128)(2,1)S(1)}, u32[]{:S(2)}, u32[]{:S(2)}) %collective-permute-start.15) | collective-permute-done | bytes 350240 | tf_op jit(solution)/shard_map/ppermute | solution.py:167
  78.3 0.9 add_convert_fusion.1
  79.1 0.8 add_convert_fusion
  82.1 1.4 %collective-permute-start.18 = (bf16[64,2736]{1,0:T(8,128)(2,1)}, bf16[64,2736]{1,0:T(8,128)(2,1)S(1)}, u32[]{:S(2)}, u32[]{:S(2)}) collective-permute-start(bf16[64,2736]{1,0:T(8,128)(2,1)} %add_convert_fusion.2), channel_id=1, source_target_pairs={{0,8},{2,10},{4,12},{6,14},{8,16},{10,18},{12,20},{14,22},{16,24},... | collective-permute-start | bytes 1050632 | tf_op jit(solution)/shard_map/ppermute | solution.py:133
  83.5 1.5 %collective-permute-start.16 = (bf16[64,2736]{1,0:T(8,128)(2,1)}, bf16[64,2736]{1,0:T(8,128)(2,1)S(1)}, u32[]{:S(2)}, u32[]{:S(2)}) collective-permute-start(bf16[64,2736]{1,0:T(8,128)(2,1)} %add_convert_fusion), channel_id=1, source_target_pairs={{0,4},{2,6},{4,0},{6,2},{8,12},{10,14},{12,8},{14,10},{16,20},{18,... | collective-permute-start | bytes 1050632 | tf_op jit(solution)/shard_map/ppermute | solution.py:167
  87.0 11.5 %collective-permute-done.17 = bf16[64,2736]{1,0:T(8,128)(2,1)S(1)} collective-permute-done((bf16[64,2736]{1,0:T(8,128)(2,1)}, bf16[64,2736]{1,0:T(8,128)(2,1)S(1)}, u32[]{:S(2)}, u32[]{:S(2)}) %collective-permute-start.17) | collective-permute-done | bytes 350240 | tf_op jit(solution)/shard_map/ppermute | solution.py:133
  98.5 14.0 %collective-permute-done.18 = bf16[64,2736]{1,0:T(8,128)(2,1)S(1)} collective-permute-done((bf16[64,2736]{1,0:T(8,128)(2,1)}, bf16[64,2736]{1,0:T(8,128)(2,1)S(1)}, u32[]{:S(2)}, u32[]{:S(2)}) %collective-permute-start.18) | collective-permute-done | bytes 350240 | tf_op jit(solution)/shard_map/ppermute | solution.py:133
  112.5 2.0 %collective-permute-done.19 = bf16[64,2736]{1,0:T(8,128)(2,1)S(1)} collective-permute-done((bf16[64,2736]{1,0:T(8,128)(2,1)}, bf16[64,2736]{1,0:T(8,128)(2,1)S(1)}, u32[]{:S(2)}, u32[]{:S(2)}) %collective-permute-start.19) | collective-permute-done | bytes 350240 | tf_op jit(solution)/shard_map/ppermute | solution.py:133
  114.5 1.2 %divide_multiply_fusion = f32[64,2736]{1,0:T(8,128)} fusion(bf16[64,2736]{1,0:T(8,128)(2,1)S(1)} %collective-permute-done.19, bf16[64,2736]{1,0:T(8,128)(2,1)S(1)} %collective-permute-done.18, bf16[64,2736]{1,0:T(8,128)(2,1)S(1)} %collective-permute-done.17, bf16[64,2736]{1,0:T(8,128)(2,1)S(1)} %collective-permute-done.16, ...), kind=kLoop, calls=%fused_computation.16 | loop fusion | flops 2276352 | bytes 3163076 | tf_op jit(solution)/shard_map/mul | solution.py:196
  (77 shorter events, 9.6 us)
Async XLA Ops:
  0.6 8.9 %copy-start.3 = (f32[1,16,1024]{2,1,0:T(8,128)S(1)}, f32[1,16,1024]{2,1,0:T(8,128)}, u32[]{:S(2)}) copy-start(f32[1,16,1024]{2,1,0:T(8,128)} %param.8) | copy-start | bytes 196612
  0.6 8.5 %copy-start = (bf16[1024,1024]{1,0:T(8,128)(2,1)S(1)}, bf16[1024,1024]{1,0:T(8,128)(2,1)}, u32[]{:S(2)}) copy-start(bf16[1024,1024]{1,0:T(8,128)(2,1)} %param.6) | copy-start | bytes 6291460
  0.7 8.7 %copy-start.2 = (f32[16,2736]{1,0:T(8,128)S(1)}, f32[16,2736]{1,0:T(8,128)}, u32[]{:S(2)}) copy-start(f32[16,2736]{1,0:T(8,128)} %param.9) | copy-start | bytes 525316
  0.7 8.8 %copy-start.4 = (s32[1024]{0:T(1024)S(1)}, s32[1024]{0:T(1024)}, u32[]{:S(2)}) copy-start(s32[1024]{0:T(1024)} %param.10) | copy-start | bytes 12292
  0.7 8.9 %collective-permute-start.4 = (f32[16,1024]{1,0:T(8,128)}, f32[16,1024]{1,0:T(8,128)S(1)}, u32[]{:S(2)}, u32[]{:S(2)}) collective-permute-start(f32[16,1024]{1,0:T(8,128)} %bitcast.15), channel_id=1, source_target_pairs={{0,1},{1,0},{2,3},{3,2},{4,5},{5,4},{6,7},{7,6},{8,9},{9,8},{10,11... | collective-permute-start | bytes 196616 | tf_op jit(solution)/shard_map/ppermute | solution.py:25
  5.1 25.2 %collective-permute-start.3 = (bf16[1024,256]{1,0:T(8,128)(2,1)}, bf16[1024,256]{1,0:T(8,128)(2,1)}, u32[]{:S(2)}, u32[]{:S(2)}) collective-permute-start(bf16[1024,256]{1,0:T(8,128)(2,1)} %get-tuple-element.62), channel_id=1, source_target_pairs={{0,1},{1,0},{2,3},{3,2},{4,5},{5,4},{6,7},{7,6},{8,9},{9,8},{10,11... | collective-permute-start | bytes 1572872 | tf_op jit(solution)/shard_map/ppermute | solution.py:25
  5.7 31.0 %collective-permute-start.2 = (bf16[1024,256]{1,0:T(8,128)(2,1)}, bf16[1024,256]{1,0:T(8,128)(2,1)}, u32[]{:S(2)}, u32[]{:S(2)}) collective-permute-start(bf16[1024,256]{1,0:T(8,128)(2,1)} %get-tuple-element.60), channel_id=1, source_target_pairs={{0,1},{1,0},{2,3},{3,2},{4,5},{5,4},{6,7},{7,6},{8,9},{9,8},{10,11... | collective-permute-start | bytes 1572872 | tf_op jit(solution)/shard_map/ppermute | solution.py:25
  7.1 47.2 %collective-permute-start.1 = (bf16[1024,256]{1,0:T(8,128)(2,1)}, bf16[1024,256]{1,0:T(8,128)(2,1)S(1)}, u32[]{:S(2)}, u32[]{:S(2)}) collective-permute-start(bf16[1024,256]{1,0:T(8,128)(2,1)} %get-tuple-element.61), channel_id=1, source_target_pairs={{0,1},{1,0},{2,3},{3,2},{4,5},{5,4},{6,7},{7,6},{8,9},{9,8},{10,11... | collective-permute-start | bytes 1572872 | tf_op jit(solution)/shard_map/ppermute | solution.py:25
  7.8 64.2 %collective-permute-start = (bf16[1024,256]{1,0:T(8,128)(2,1)}, bf16[1024,256]{1,0:T(8,128)(2,1)}, u32[]{:S(2)}, u32[]{:S(2)}) collective-permute-start(bf16[1024,256]{1,0:T(8,128)(2,1)} %get-tuple-element.59), channel_id=1, source_target_pairs={{0,1},{1,0},{2,3},{3,2},{4,5},{5,4},{6,7},{7,6},{8,9},{9,8},{10,11... | collective-permute-start | bytes 1572872 | tf_op jit(solution)/shard_map/ppermute | solution.py:25
  27.6 5.7 %slice-start = ((s8[5603328]{0:T(1024)(128)(4,1)}), s8[4194304]{0:T(1024)(128)(4,1)S(1)}, s32[]{:S(2)}) async-start(s8[5603328]{0:T(1024)(128)(4,1)} %bitcast.13), calls=%async_computation | async-start | bytes 8388608
  27.6 5.7 %slice-start.1 = ((s8[5603328]{0:T(1024)(128)(4,1)}), s8[1409024]{0:T(1024)(128)(4,1)S(1)}, s32[]{:S(2)}) async-start(s8[5603328]{0:T(1024)(128)(4,1)} %bitcast.13), calls=%async_computation.1 | async-start | bytes 2818048
  27.6 15.0 %collective-permute-start.20 = (f32[3760]{0:T(1024)S(1)}, f32[3760]{0:T(1024)S(1)}, u32[]{:S(2)}, u32[]{:S(2)}) collective-permute-start(f32[3760]{0:T(1024)S(1)} %maximum_convert_fusion), channel_id=1, source_target_pairs={{0,16},{2,18},{4,20},{6,22},{8,24},{10,26},{12,28},{14,30},{16,0},... | collective-permute-start | bytes 45128 | tf_op jit(solution)/shard_map/ppermute | solution.py:145
  33.2 2.9 %collective-permute-start.5 = (bf16[64,2736]{1,0:T(8,128)(2,1)S(1)}, bf16[64,2736]{1,0:T(8,128)(2,1)S(1)}, u32[]{:S(2)}, u32[]{:S(2)}) collective-permute-start(bf16[64,2736]{1,0:T(8,128)(2,1)S(1)} %get-tuple-element.58), channel_id=1, source_target_pairs={{0,2},{2,0},{4,6},{6,4},{8,10},{10,8},{12,14},{14,12},{16,18},{18,... | collective-permute-start | bytes 1050632 | tf_op jit(solution)/shard_map/ppermute | solution.py:118
  36.1 8.1 %collective-permute-start.7 = (bf16[64,2736]{1,0:T(8,128)(2,1)S(1)}, bf16[64,2736]{1,0:T(8,128)(2,1)S(1)}, u32[]{:S(2)}, u32[]{:S(2)}) collective-permute-start(bf16[64,2736]{1,0:T(8,128)(2,1)S(1)} %get-tuple-element.57), channel_id=1, source_target_pairs={{0,2},{2,0},{4,6},{6,4},{8,10},{10,8},{12,14},{14,12},{16,18},{18,... | collective-permute-start | bytes 1050632 | tf_op jit(solution)/shard_map/ppermute | solution.py:118
  39.7 5.0 %collective-permute-start.6 = (bf16[64,2736]{1,0:T(8,128)(2,1)S(1)}, bf16[64,2736]{1,0:T(8,128)(2,1)S(1)}, u32[]{:S(2)}, u32[]{:S(2)}) collective-permute-start(bf16[64,2736]{1,0:T(8,128)(2,1)S(1)} %get-tuple-element.56), channel_id=1, source_target_pairs={{0,2},{2,0},{4,6},{6,4},{8,10},{10,8},{12,14},{14,12},{16,18},{18,... | collective-permute-start | bytes 1050632 | tf_op jit(solution)/shard_map/ppermute | solution.py:118
  42.6 10.9 %collective-permute-start.8 = (bf16[64,2736]{1,0:T(8,128)(2,1)S(1)}, bf16[64,2736]{1,0:T(8,128)(2,1)S(1)}, u32[]{:S(2)}, u32[]{:S(2)}) collective-permute-start(bf16[64,2736]{1,0:T(8,128)(2,1)S(1)} %add_convert_fusion.6), channel_id=1, source_target_pairs={{0,4},{2,6},{4,0},{6,2},{8,12},{10,14},{12,8},{14,10},{16,20},{18,... | collective-permute-start | bytes 1050632 | tf_op jit(solution)/shard_map/ppermute | solution.py:167
  44.2 16.7 %collective-permute-start.21 = (f32[3760]{0:T(1024)S(1)}, f32[3760]{0:T(1024)S(1)}, u32[]{:S(2)}, u32[]{:S(2)}) collective-permute-start(f32[3760]{0:T(1024)S(1)} %fusion.29), channel_id=1, source_target_pairs={{0,8},{2,10},{4,12},{6,14},{8,0},{10,2},{12,4},{14,6},{16,24},{18,... | collective-permute-start | bytes 45128 | tf_op jit(solution)/shard_map/ppermute | solution.py:145
  44.7 16.8 %collective-permute-start.10 = (bf16[64,2736]{1,0:T(8,128)(2,1)S(1)}, bf16[64,2736]{1,0:T(8,128)(2,1)S(1)}, u32[]{:S(2)}, u32[]{:S(2)}) collective-permute-start(bf16[64,2736]{1,0:T(8,128)(2,1)S(1)} %get-tuple-element.55), channel_id=1, source_target_pairs={{0,2},{2,0},{4,6},{6,4},{8,10},{10,8},{12,14},{14,12},{16,18},{18,... | collective-permute-start | bytes 1050632 | tf_op jit(solution)/shard_map/ppermute | solution.py:118
  56.4 5.1 %collective-permute-start.9 = (bf16[64,2736]{1,0:T(8,128)(2,1)S(1)}, bf16[64,2736]{1,0:T(8,128)(2,1)S(1)}, u32[]{:S(2)}, u32[]{:S(2)}) collective-permute-start(bf16[64,2736]{1,0:T(8,128)(2,1)S(1)} %get-tuple-element.54), channel_id=1, source_target_pairs={{0,2},{2,0},{4,6},{6,4},{8,10},{10,8},{12,14},{14,12},{16,18},{18,... | collective-permute-start | bytes 1050632 | tf_op jit(solution)/shard_map/ppermute | solution.py:118
  59.3 11.7 %collective-permute-start.11 = (bf16[64,2736]{1,0:T(8,128)(2,1)S(1)}, bf16[64,2736]{1,0:T(8,128)(2,1)S(1)}, u32[]{:S(2)}, u32[]{:S(2)}) collective-permute-start(bf16[64,2736]{1,0:T(8,128)(2,1)S(1)} %add_convert_fusion.5), channel_id=1, source_target_pairs={{0,4},{2,6},{4,0},{6,2},{8,12},{10,14},{12,8},{14,10},{16,20},{18,... | collective-permute-start | bytes 1050632 | tf_op jit(solution)/shard_map/ppermute | solution.py:167
  60.9 10.1 %collective-permute-start.22 = (f32[3760]{0:T(1024)S(1)}, f32[3760]{0:T(1024)S(1)}, u32[]{:S(2)}, u32[]{:S(2)}) collective-permute-start(f32[3760]{0:T(1024)S(1)} %max.62), channel_id=1, source_target_pairs={{0,4},{2,6},{4,0},{6,2},{8,12},{10,14},{12,8},{14,10},{16,20},{18,... | collective-permute-start | bytes 45128 | tf_op jit(solution)/shard_map/ppermute | solution.py:145
  61.5 14.6 %collective-permute-start.14 = (bf16[64,2736]{1,0:T(8,128)(2,1)S(1)}, bf16[64,2736]{1,0:T(8,128)(2,1)S(1)}, u32[]{:S(2)}, u32[]{:S(2)}) collective-permute-start(bf16[64,2736]{1,0:T(8,128)(2,1)S(1)} %get-tuple-element.53), channel_id=1, source_target_pairs={{0,2},{2,0},{4,6},{6,4},{8,10},{10,8},{12,14},{14,12},{16,18},{18,... | collective-permute-start | bytes 1050632 | tf_op jit(solution)/shard_map/ppermute | solution.py:118
  61.6 16.7 %collective-permute-start.15 = (bf16[64,2736]{1,0:T(8,128)(2,1)S(1)}, bf16[64,2736]{1,0:T(8,128)(2,1)S(1)}, u32[]{:S(2)}, u32[]{:S(2)}) collective-permute-start(bf16[64,2736]{1,0:T(8,128)(2,1)S(1)} %add_convert_fusion.3), channel_id=1, source_target_pairs={{0,4},{2,6},{4,0},{6,2},{8,12},{10,14},{12,8},{14,10},{16,20},{18,... | collective-permute-start | bytes 1050632 | tf_op jit(solution)/shard_map/ppermute | solution.py:167
  71.0 8.9 %collective-permute-start.23 = (f32[3760]{0:T(1024)S(1)}, f32[3760]{0:T(1024)S(1)}, u32[]{:S(2)}, u32[]{:S(2)}) collective-permute-start(f32[3760]{0:T(1024)S(1)} %max.63), channel_id=1, source_target_pairs={{0,2},{2,0},{4,6},{6,4},{8,10},{10,8},{12,14},{14,12},{16,18},{18,... | collective-permute-start | bytes 45128 | tf_op jit(solution)/shard_map/ppermute | solution.py:145
  71.9 14.4 %slice-start.2 = ((s32[6496]{0:T(1024)}), s32[1024]{0:T(1024)S(1)}, s32[]{:S(2)}) async-start(s32[6496]{0:T(1024)} %param.11), calls=%async_computation.2 | async-start | bytes 8192 | tf_op jit(solution)/shard_map/slice | solution.py:197
  75.6 3.5 %collective-permute-start.13 = (bf16[64,2736]{1,0:T(8,128)(2,1)S(1)}, bf16[64,2736]{1,0:T(8,128)(2,1)S(1)}, u32[]{:S(2)}, u32[]{:S(2)}) collective-permute-start(bf16[64,2736]{1,0:T(8,128)(2,1)S(1)} %get-tuple-element.52), channel_id=1, source_target_pairs={{0,2},{2,0},{4,6},{6,4},{8,10},{10,8},{12,14},{14,12},{16,18},{18,... | collective-permute-start | bytes 1050632 | tf_op jit(solution)/shard_map/ppermute | solution.py:118
  76.1 8.9 %collective-permute-start.12 = (bf16[64,2736]{1,0:T(8,128)(2,1)}, bf16[64,2736]{1,0:T(8,128)(2,1)S(1)}, u32[]{:S(2)}, u32[]{:S(2)}) collective-permute-start(bf16[64,2736]{1,0:T(8,128)(2,1)} %get-tuple-element.51), channel_id=1, source_target_pairs={{0,2},{2,0},{4,6},{6,4},{8,10},{10,8},{12,14},{14,12},{16,18},{18,... | collective-permute-start | bytes 1050632 | tf_op jit(solution)/shard_map/ppermute | solution.py:118
  80.0 5.6 %collective-permute-start.24 = (f32[1024]{0:T(1024)S(1)}, f32[1024]{0:T(1024)S(1)}, u32[]{:S(2)}, u32[]{:S(2)}) collective-permute-start(f32[1024]{0:T(1024)S(1)} %slice.12), channel_id=1, source_target_pairs={{0,1},{1,0},{2,3},{3,2},{4,5},{5,4},{6,7},{7,6},{8,9},{9,8},{10,11... | collective-permute-start | bytes 12296 | tf_op jit(solution)/shard_map/ppermute | solution.py:34
  81.5 17.0 %collective-permute-start.17 = (bf16[64,2736]{1,0:T(8,128)(2,1)}, bf16[64,2736]{1,0:T(8,128)(2,1)S(1)}, u32[]{:S(2)}, u32[]{:S(2)}) collective-permute-start(bf16[64,2736]{1,0:T(8,128)(2,1)} %add_convert_fusion.4), channel_id=1, source_target_pairs={{0,16},{2,18},{4,20},{6,22},{8,24},{10,26},{12,28},{14,30},{16,0},... | collective-permute-start | bytes 1050632 | tf_op jit(solution)/shard_map/ppermute | solution.py:133
  82.1 30.4 %collective-permute-start.18 = (bf16[64,2736]{1,0:T(8,128)(2,1)}, bf16[64,2736]{1,0:T(8,128)(2,1)S(1)}, u32[]{:S(2)}, u32[]{:S(2)}) collective-permute-start(bf16[64,2736]{1,0:T(8,128)(2,1)} %add_convert_fusion.2), channel_id=1, source_target_pairs={{0,8},{2,10},{4,12},{6,14},{8,16},{10,18},{12,20},{14,22},{16,24},... | collective-permute-start | bytes 1050632 | tf_op jit(solution)/shard_map/ppermute | solution.py:133
  83.5 29.0 %collective-permute-start.16 = (bf16[64,2736]{1,0:T(8,128)(2,1)}, bf16[64,2736]{1,0:T(8,128)(2,1)S(1)}, u32[]{:S(2)}, u32[]{:S(2)}) collective-permute-start(bf16[64,2736]{1,0:T(8,128)(2,1)} %add_convert_fusion), channel_id=1, source_target_pairs={{0,4},{2,6},{4,0},{6,2},{8,12},{10,14},{12,8},{14,10},{16,20},{18,... | collective-permute-start | bytes 1050632 | tf_op jit(solution)/shard_map/ppermute | solution.py:167
  85.0 29.6 %collective-permute-start.19 = (bf16[64,2736]{1,0:T(8,128)(2,1)}, bf16[64,2736]{1,0:T(8,128)(2,1)S(1)}, u32[]{:S(2)}, u32[]{:S(2)}) collective-permute-start(bf16[64,2736]{1,0:T(8,128)(2,1)} %add_convert_fusion.1), channel_id=1, source_target_pairs={{0,24},{2,26},{4,28},{6,30},{8,0},{10,2},{12,4},{14,6},{16,8},{18,... | collective-permute-start | bytes 1050632 | tf_op jit(solution)/shard_map/ppermute | solution.py:133
  (1 other events, 2.4 us)
